TPU v7x, 8 devices: a whole 2x2x1 slice. The times are simulated.
8 devices in a mesh: dp: 2 (over z, y), tp: 4 (over x, core).
Axes of the slice: x: 2, y: 2, z: 1, core: 2. Of those that a mesh axis runs over, the one named last changes fastest.
Arguments:
- hidden: bfloat16 [8, 5, 2048], P('dp'), parts along dimension 0
- norm_gain: float32 [2048], replicated
- w_head: bfloat16 [2048, 151936], P(None, 'tp')
- draft_probs: float32 [8, 4, 151936], P('dp', None, 'tp'), parts along dimension 0
- draft_tokens: int32 [8, 4], P('dp'), parts along dimension 0
- temperature: float32 [8], P('dp'), parts along dimension 0
Outputs:
- output 1: float32 [8, 4], P('dp'), parts along dimension 0
- output 2: float32 [8, 4], P('dp'), parts along dimension 0
- output 3: float32 [8, 4, 151936], P('dp', None, 'tp'), parts along dimension 0
- output 4: float32 [8], P('dp'), parts along dimension 0
There are 2 independent parts. A program takes and returns all parts, laid end to end along the dimension named above; an argument that names none is the same for every part.
All inputs are finite; a program needn't handle non-finite values.
Results may differ from a plain program's by a relative error of at most 0.001.
Values sent between devices are 32-bit elements.
A program may use at most 1 GiB of HBM per device.

v0:
```python
import jax
import jax.numpy as jnp
from jax import lax
from jax.experimental import pallas as pl
from jax.experimental.pallas import tpu as pltpu
from jax.sharding import PartitionSpec as P

MESH = pl.DeviceIdType.MESH
F32 = jnp.float32
LOWEST = float(jnp.finfo(jnp.float32).min)

TILE = 1024
SUB = 256
DEPTH = 256
SLOTS = 3
SHARED = 14
FIRST = 6
HELD = 2
RELAY = 4
PARTS = 2
PASS = 2048


def verify_kernel(
    h_hbm, g_hbm, t_hbm, dt_hbm, w_ref, q_ref,
    ex_ref, norm_ref, acc_ref, lse_ref,
    h_ref, g_ref, t_ref, dt_ref, wbuf, wtail, qv, s_scr, xf, xp, xrows, xb, xt, tv, tp_recv, ct, dl, m_scr, l_scr, k_scr,
    zsend, pstat_s, pstat_r, e1s, e1r, e2s, e2r, e3s, e3r,
    in_sem, w_sem, wt_sem, q_sem, x_sem, t_sem, zs_sem, zr_sem, ps_sem, e1_sem, e2_sem, e3_sem,
):
    dp, tp = lax.axis_index("dp"), lax.axis_index("tp")
    partner = (1 - dp, tp)
    peers = [(dp, lax.rem(tp + d, 4)) for d in (1, 2, 3)]
    n_ids, width = w_ref.shape
    n_full = n_ids // TILE
    tail = n_ids - n_full * TILE
    tail_at = n_full * TILE
    last = n_full - 2 * SHARED - FIRST
    steps = FIRST + SHARED + last

    def column(i):
        in_shared = (i + steps - FIRST) // steps
        past_shared = (i + steps - FIRST - SHARED) // steps
        return pl.multiple_of((i + in_shared * dp * SHARED + past_shared * (SHARED - dp * SHARED)) * TILE, TILE)

    part = TILE // PARTS

    def tile_copies(i, slot):
        at = column(i)
        return [
            pltpu.make_async_copy(
                w_ref.at[pl.ds(at + k * part, part), :], wbuf.at[slot, pl.ds(k * part, part), :], w_sem.at[slot, k]
            )
            for k in range(PARTS)
        ]

    tail_copy = pltpu.make_async_copy(w_ref.at[pl.ds(tail_at, tail), :], wtail, wt_sem)
    q_copy = pltpu.make_async_copy(q_ref, qv, q_sem)
    small = [
        pltpu.make_async_copy(src, dst, in_sem.at[k])
        for k, (src, dst) in enumerate(((h_hbm, h_ref), (g_hbm, g_ref), (t_hbm, t_ref), (dt_hbm, dt_ref)))
    ]
    for c in small:
        c.start()
    tail_copy.start()
    for c in tile_copies(0, 0):
        c.start()

    barrier = pltpu.get_barrier_semaphore()
    for other in [partner] + peers:
        pl.semaphore_signal(barrier, inc=1, device_id=other, device_id_type=MESH)

    for c in small:
        c.wait()
    for c in tile_copies(1, 1):
        c.start()
    h = h_ref[...].astype(F32)
    inv_rms = lax.rsqrt(jnp.mean(h * h, axis=-1, keepdims=True) + 1e-5)
    xf[...] = h * inv_rms * g_ref[...][None]
    for b in range(4):
        tv[0, b : b + 1, :] = jnp.full((1, 128), 1.0, F32) / jnp.full((1, 128), t_ref[b], F32)
        for j in range(4):
            tv[1 + j, b : b + 1, :] = jnp.full((1, 128), dt_ref[b, j].astype(F32), F32)

    def lay_rows(src, t_src, at):
        xrows[...] = jnp.zeros_like(xrows)
        lane = lax.broadcasted_iota(jnp.int32, (1, 128), 1) + tp * n_ids
        for b in range(4):
            for j in range(5):
                xrows[8 * b + j : 8 * b + j + 1, :] = src[j, b : b + 1, :]
            ct[at + 8 * b : at + 8 * b + 8, :] = jnp.broadcast_to(t_src[0, b : b + 1, :], (8, 128))
            dl[at + 8 * b : at + 8 * b + 8, :] = jnp.full((8, 128), -1.0, F32)
            for j in range(4):
                dl[at + 8 * b + j : at + 8 * b + j + 1, :] = t_src[1 + j, b : b + 1, :] - lane.astype(F32)
        rows = xrows[...].astype(jnp.bfloat16)
        xb[at : at + 32, :] = rows
        for k in range(0, width, 128):
            xt[k : k + 128, at : at + 32] = xrows[:, k : k + 128].T.astype(jnp.bfloat16)

    xt[:, 32:128] = jnp.zeros((width, 96), jnp.bfloat16)
    xb[32:64, :] = jnp.zeros((32, width), jnp.bfloat16)
    lay_rows(xf, tv, 0)
    for i in range(2, SLOTS):
        for c in tile_copies(i, i):
            c.start()
    m_scr[...] = jnp.full(m_scr.shape, LOWEST, F32)
    l_scr[...] = jnp.zeros_like(l_scr)
    k_scr[...] = jnp.zeros_like(k_scr)

    pl.semaphore_wait(barrier, 4)
    core = lax.rem(tp, 2)
    sibling = (dp, tp + 1 - 2 * core)

    def width_half(ref, c):
        return ref.at[:, :, pl.ds(pl.multiple_of(c * (width // 2), width // 2), width // 2)]

    def x_copy(src, c, to, k):
        return pltpu.make_async_remote_copy(
            src_ref=width_half(src, c), dst_ref=width_half(xp, c), send_sem=x_sem.at[0, k], recv_sem=x_sem.at[1, k],
            device_id=to, device_id_type=MESH,
        )

    x_direct = x_copy(xf, core, partner, 0)
    x_relay = x_copy(xp, core, sibling, 1)
    t_copy = pltpu.make_async_remote_copy(
        src_ref=tv, dst_ref=tp_recv, send_sem=t_sem.at[0], recv_sem=t_sem.at[1], device_id=partner, device_id_type=MESH
    )
    x_direct.start()
    t_copy.start()

    def by_rows(w, depth):
        return lax.dot_general(xb[:, depth], w, (((1,), (1,)), ((), ())), preferred_element_type=F32)

    def by_ids(w, depth):
        return lax.dot_general(w, xt[depth, :], (((1,), (0,)), ((), ())), preferred_element_type=F32)

    def products(slot, lo, size):
        block = min(SUB, size // 2)
        starts = range(lo, lo + size, block)
        fixed = len(starts) // 2
        sums = [None] * len(starts)
        for k in range(0, width, DEPTH):
            depth = slice(k, k + DEPTH)
            for n, start in enumerate(starts):
                w = wbuf[slot, start : start + block, depth]
                z = by_rows(w, depth) if n < fixed else by_ids(w, depth)
                sums[n] = z if k == 0 else sums[n] + z
        pieces = []
        for n, z in enumerate(sums):
            for at in range(0, block, 128):
                pieces.append(z[:, at : at + 128] if n < fixed else z[at : at + 128, :].T[0:64])
        return pieces

    def fold(rows, parts):
        m_old = m_scr[0:rows, :]
        m_new = m_old
        for p in parts:
            m_new = jnp.maximum(m_new, p)
        total = l_scr[0:rows, :] * jnp.exp(m_old - m_new)
        for p in parts:
            total = total + jnp.exp(p - m_new)
        m_scr[0:rows, :] = m_new
        l_scr[0:rows, :] = total

    tail_copy.wait()
    s = by_rows(wtail[...], slice(0, width))[0:32] * ct[0:32, 0:tail]
    for b in range(4):
        s_scr[b, :, tail_at : tail_at + tail] = s[8 * b : 8 * b + 4, :]
    k_scr[0:32, 0:tail] = jnp.where(dl[0:32, 0:tail] == float(tail_at), s, 0.0)
    m_tail = jnp.max(s, axis=1, keepdims=True)
    l_tail = jnp.sum(jnp.exp(s - m_tail), axis=1, keepdims=True)
    lane0 = lax.broadcasted_iota(jnp.int32, (32, 128), 1) == 0
    m_scr[0:32, :] = jnp.where(lane0, m_tail, LOWEST)
    l_scr[0:32, :] = jnp.where(lane0, l_tail, 0.0)

    def z_copy(k):
        at = column(FIRST + k)
        return pltpu.make_async_remote_copy(
            src_ref=zsend.at[k], dst_ref=s_scr.at[:, :, pl.ds(at, TILE)], send_sem=zs_sem.at[k], recv_sem=zr_sem.at[k],
            device_id=partner, device_id_type=MESH,
        )

    def consume(slot, at, lo, size, rows, k):
        kept = k_scr[0:rows, :]
        parts = []
        for n, z in enumerate(products(slot, lo, size)):
            s = z[0:rows] * ct[0:rows, :]
            parts.append(s)
            off = lo + n * 128
            kept = jnp.where(dl[0:rows, :] == (at + off).astype(F32), s, kept)
            for b in range(4):
                s_scr[b, :, pl.ds(at + off, 128)] = s[8 * b : 8 * b + 4, :]
                if rows == 64:
                    zsend[k, b, :, off : off + 128] = s[32 + 8 * b : 32 + 8 * b + 4, :]
            if n % 2:
                fold(rows, parts)
                parts = []
        k_scr[0:rows, :] = kept

    def step(i, rows):
        slot = i % SLOTS
        for c in tile_copies(i, slot):
            c.wait()
        k = i - FIRST
        consume(slot, column(i), 0, TILE, rows, k)

        @pl.when(i + SLOTS < steps)
        def _():
            for c in tile_copies(i + SLOTS, slot):
                c.start()

        if rows == 64:

            @pl.when(k < SHARED - HELD)
            def _():
                z_copy(k).start()

    group = lax.broadcasted_iota(jnp.int32, (8, 128), 1) // 32

    def pack(cols):
        size = cols[0].shape[0]
        packed = jnp.broadcast_to(cols[0], (size, 128))
        for b in range(1, 4):
            packed = jnp.where(group[:size] == b, cols[b], packed)
        return packed

    def unpack(packed, b):
        size = packed.shape[0]
        lane = lax.broadcasted_iota(jnp.int32, (size, 128), 1)
        return jnp.sum(jnp.where(lane == 32 * b, packed, 0.0), axis=1, keepdims=True)

    def packed_lse(at):
        m = m_scr[at : at + 32, :]
        top = jnp.max(m, axis=1, keepdims=True)
        lse = top + jnp.log(jnp.sum(l_scr[at : at + 32, :] * jnp.exp(m - top), axis=1, keepdims=True))
        return pack([lse[8 * b : 8 * b + 8, :] for b in range(4)])

    def packed_token(at):
        kept = jnp.sum(k_scr[at : at + 32, :], axis=1, keepdims=True)
        return pack([kept[8 * b : 8 * b + 8, :] for b in range(4)])

    lax.fori_loop(0, RELAY, lambda i, _: step(i, 32), None)
    x_direct.wait()
    x_relay.start()
    lax.fori_loop(RELAY, FIRST, lambda i, _: step(i, 32), None)
    x_copy(xp, 1 - core, sibling, 1).wait_recv()
    x_relay.wait_send()
    t_copy.wait()
    lay_rows(xp, tp_recv, 32)
    lax.fori_loop(FIRST, FIRST + SHARED, lambda i, _: step(i, 64), None)
    q_copy.start()
    pstat_s[0] = packed_lse(32)
    pstat_s[1] = packed_token(32)
    stat_copy = pltpu.make_async_remote_copy(
        src_ref=pstat_s, dst_ref=pstat_r, send_sem=ps_sem.at[0], recv_sem=ps_sem.at[1],
        device_id=partner, device_id_type=MESH,
    )
    stat_copy.start()
    for k in range(SHARED - HELD, SHARED):
        z_copy(k).start()
    lax.fori_loop(FIRST + SHARED, steps - 1, lambda i, _: step(i, 32), None)
    end, slot = steps - 1, (steps - 1) % SLOTS
    copies = tile_copies(end, slot)
    for lo, size in ((0, part), (part, part)):
        for c in copies[lo // part : (lo + size) // part]:
            c.wait()
        consume(slot, column(end), lo, size, 32, 0)

    def exchange(src, dst, sem):
        return [
            pltpu.make_async_remote_copy(
                src_ref=src, dst_ref=dst.at[d], send_sem=sem.at[0, d], recv_sem=sem.at[1, d],
                device_id=peers[d], device_id_type=MESH,
            )
            for d in range(3)
        ]

    mine = packed_lse(0)
    stat_copy.wait()
    theirs = pstat_r[0]
    top = jnp.maximum(mine, theirs)
    near = top + jnp.log(jnp.exp(mine - top) + jnp.exp(theirs - top))
    e1s[...] = near
    e1 = exchange(e1s, e1r, e1_sem)
    for c in e1:
        c.start()

    own = [dl[8 * b : 8 * b + 4, :] for b in range(4)]

    row_m = [jnp.broadcast_to(unpack(near[0:4, :], b), (4, 128)) for b in range(4)]

    def prepare(at, size):
        places = [(b, at + off, min(size, 128)) for b in range(4) for off in range(0, size, 128)]
        values = [s_scr[b, :, pl.ds(a, n)] for b, a, n in places]
        values = [jnp.exp(v - row_m[b][:, :n]) for v, (b, _, n) in zip(values, places)]
        for v, (b, a, n) in zip(values, places):
            s_scr[b, :, pl.ds(a, n)] = v

    def pick(at, size, found):
        out = []
        for b in range(4):
            f = found[b]
            for off in range(0, size, 128):
                n = min(size, 128)
                f = jnp.where(own[b][:, :n] == jnp.asarray(at + off).astype(F32), qv[b, :, pl.ds(at + off, n)], f)
            out.append(f)
        return tuple(out)

    zero = jnp.zeros((4, 128), F32)
    lax.fori_loop(0, steps, lambda i, _: prepare(column(i), TILE), None)
    prepare(tail_at, tail)
    q_copy.wait()
    whole = tail_at // PASS * PASS
    found = lax.fori_loop(0, whole // PASS, lambda i, f: pick(pl.multiple_of(i * PASS, 128), PASS, f), (zero,) * 4)
    found = pick(whole, tail_at - whole, found)
    found_tail = pick(tail_at, tail, (jnp.zeros((4, tail), F32),) * 4)
    token_q = []
    for b in range(4):
        f = found_tail[b]
        token_q.append(jnp.sum(found[b], axis=1, keepdims=True) + jnp.sum(f, axis=1, keepdims=True))
    e3s[0] = (packed_token(0) + pstat_r[1])[0:4, :]
    e3s[1] = pack(token_q)
    e3 = exchange(e3s, e3r, e3_sem)
    for c in e3:
        c.start()

    def take_z(k, _):
        z_copy(k).wait_send()
        at = pl.multiple_of((FIRST + (1 - dp) * SHARED + k) * TILE, TILE)
        pltpu.make_async_remote_copy(
            src_ref=zsend.at[k], dst_ref=s_scr.at[:, :, pl.ds(at, TILE)], send_sem=zs_sem.at[k], recv_sem=zr_sem.at[k],
            device_id=partner, device_id_type=MESH,
        ).wait_recv()
        prepare(at, TILE)

    lax.fori_loop(0, SHARED, take_z, None)

    for c in e1:
        c.wait()
    lses = [near] + [e1r[d] for d in range(3)]
    top = jnp.maximum(jnp.maximum(lses[0], lses[1]), jnp.maximum(lses[2], lses[3]))
    sums = jnp.exp(lses[0] - top) + jnp.exp(lses[1] - top) + jnp.exp(lses[2] - top) + jnp.exp(lses[3] - top)
    lse = top + jnp.log(sums)
    lse_ref[...] = lse
    scale = [jnp.exp(row_m[b] - jnp.broadcast_to(unpack(lse[0:4, :], b), (4, 128))) for b in range(4)]

    def excess(b, at, size):
        e = jnp.maximum(s_scr[b, :, pl.ds(at, size)] * scale[b][:, :size] - qv[b, :, pl.ds(at, size)], 0.0)
        ex_ref[b, :, pl.ds(at, size)] = e
        return e

    def last_pass(at, size, sums):
        out = []
        for b in range(4):
            acc = sums[b]
            for off in range(0, size, 128):
                acc = acc + excess(b, at + off, 128)
            out.append(acc)
        return tuple(out)

    sums = lax.fori_loop(0, whole // PASS, lambda i, t: last_pass(pl.multiple_of(i * PASS, 128), PASS, t), (zero,) * 4)
    sums = last_pass(whole, tail_at - whole, sums)
    rows = []
    for b in range(4):
        e = excess(b, tail_at, tail)
        rows.append(jnp.sum(sums[b], axis=1, keepdims=True) + jnp.sum(e, axis=1, keepdims=True))
    e2s[...] = pack(rows)
    e2 = exchange(e2s, e2r, e2_sem)
    for c in e2:
        c.start()

    for c in e3:
        c.wait()
    at_token = (e3s[...] + e3r[0]) + (e3r[1] + e3r[2])
    acc_ref[...] = jnp.minimum(jnp.exp(at_token[0] - lse[0:4, :]) / at_token[1], 1.0)

    for c in e2:
        c.wait()
    norm_ref[...] = (e2s[...] + e2r[0]) + (e2r[1] + e2r[2])


def finish_kernel(
    ex_ref, norm_ref, acc_ref, lse_ref, acc_out, norm_out, res_out, bonus_out, acc_v, norm_v, bonus_v, stage, sem, r_sem
):
    n_ids = ex_ref.shape[2]
    lane = lax.broadcasted_iota(jnp.int32, (4, 128), 1)
    norm = norm_ref[...]
    writes = []
    for b in range(4):
        total = jnp.sum(jnp.where(lane == 32 * b, norm, 0.0), axis=1, keepdims=True)
        scale = jnp.broadcast_to(1.0 / jnp.broadcast_to(total, (4, 128)), (4, 128))

        for at in range(0, n_ids, 128):
            size = min(128, n_ids - at)
            stage[b, :, at : at + size] = ex_ref[b, :, at : at + size] * scale[:, :size]
        writes.append(pltpu.make_async_copy(stage.at[b], res_out.at[b], r_sem.at[b]))
        writes[-1].start()

    sub = lax.broadcasted_iota(jnp.int32, (4, 128), 0)
    for src, dst, out, k in ((acc_ref[...], acc_v, acc_out, 0), (norm, norm_v, norm_out, 1)):
        row = jnp.sum(jnp.where(lane % 32 == sub, src, 0.0), axis=0, keepdims=True)
        for b in range(4):
            dst[b : b + 1, :] = (row if b == 0 else pltpu.roll(row, 128 - 32 * b, 1))[:, 0:4]
        writes.append(pltpu.make_async_copy(dst, out, sem.at[k]))
        writes[-1].start()
    row = lse_ref[4:5, :]
    lane = lane[0:1, :]
    packed = row
    for b in range(1, 4):
        packed = jnp.where(lane == b, pltpu.roll(row, 128 - 31 * b, 1), packed)
    bonus_v[...] = packed[:, 0:4]
    writes.append(pltpu.make_async_copy(bonus_v, bonus_out, sem.at[2]))
    writes[-1].start()
    for c in writes:
        c.wait()


def solution(mesh):
    def local_step(hidden, norm_gain, w_head, draft_probs, draft_tokens, temperature):
        n_ids = w_head.shape[1]
        width = w_head.shape[0]
        pad_ids = -(-n_ids // 128) * 128
        tail = n_ids % TILE
        vmem, smem, hbm = pltpu.VMEM, pltpu.SMEM, pltpu.HBM
        dma = pltpu.SemaphoreType.DMA
        ex, norm, acc, lse = pl.pallas_call(
            verify_kernel,
            out_shape=[vmem((4, 4, n_ids), F32), vmem((4, 128), F32), vmem((4, 128), F32), vmem((8, 128), F32)],
            in_specs=[pl.BlockSpec(memory_space=s) for s in (hbm,) * 6],
            out_specs=[pl.BlockSpec(memory_space=vmem)] * 4,
            scratch_shapes=[
                vmem((5, 4, width), jnp.bfloat16),
                vmem((1, width), F32),
                smem((4,), F32),
                smem((4, 4), jnp.int32),
                vmem((SLOTS, TILE, width), jnp.bfloat16),
                vmem((tail, width), jnp.bfloat16),
                vmem((4, 4, n_ids), F32),
                vmem((4, 4, pad_ids), F32),
                vmem((5, 4, width), F32),
                vmem((5, 4, width), F32),
                vmem((32, width), F32),
                vmem((64, width), jnp.bfloat16),
                vmem((width, 128), jnp.bfloat16),
                vmem((5, 4, 128), F32),
                vmem((5, 4, 128), F32),
                vmem((64, 128), F32),
                vmem((64, 128), F32),
                vmem((64, 128), F32),
                vmem((64, 128), F32),
                vmem((64, 128), F32),
                vmem((SHARED, 4, 4, TILE), F32),
                vmem((2, 8, 128), F32),
                vmem((2, 8, 128), F32),
                vmem((8, 128), F32),
                vmem((3, 8, 128), F32),
                vmem((4, 128), F32),
                vmem((3, 4, 128), F32),
                vmem((2, 4, 128), F32),
                vmem((3, 2, 4, 128), F32),
                dma((4,)), dma((SLOTS, PARTS)), dma, dma, dma((2, 2)), dma((2,)), dma((SHARED,)), dma((SHARED,)), dma((2,)),
                dma((2, 3)), dma((2, 3)), dma((2, 3)),
            ],
            compiler_params=pltpu.CompilerParams(collective_id=0, has_side_effects=True),
            name="verify",
        )(
            hidden.transpose(1, 0, 2), norm_gain.reshape(1, width), temperature, draft_tokens,
            w_head.T, draft_probs,
        )
        acc, norm, residual, bonus = pl.pallas_call(
            finish_kernel,
            out_shape=[
                jax.ShapeDtypeStruct((4, 4), F32),
                jax.ShapeDtypeStruct((4, 4), F32),
                jax.ShapeDtypeStruct((4, 4, n_ids), F32),
                jax.ShapeDtypeStruct((1, 4), F32),
            ],
            in_specs=[pl.BlockSpec(memory_space=vmem)] * 4,
            out_specs=[pl.BlockSpec(memory_space=hbm)] * 4,
            scratch_shapes=[
                vmem((4, 4), F32), vmem((4, 4), F32), vmem((1, 4), F32), vmem((4, 4, n_ids), F32), dma((3,)), dma((4,)),
            ],
            compiler_params=pltpu.CompilerParams(vmem_limit_bytes=16 * 1024 * 1024),
            name="finish",
        )(ex, norm, acc, lse)
        return acc, norm, residual, bonus.reshape(4)

    return jax.shard_map(
        local_step,
        mesh=mesh,
        in_specs=(P("dp", None, None), P(), P(None, "tp"), P("dp", None, "tp"), P("dp", None), P("dp")),
        out_specs=(P("dp", None), P("dp", None), P("dp", None, "tp"), P("dp")),
        check_vma=False,
    )
```

profile of v0, /device:TPU:0, one launch (start us, length us, event | category | flops | bytes accessed | tf_op | source)
XLA Modules:
  0.0 42.8 jit_solution(3478234937042110550)
XLA Ops:
  0.6 40.5 %verify.1 = (f32[4,4,37984]{2,1,0:T(4,128)S(1)}, f32[4,128]{1,0:T(4,128)S(1)}, f32[4,128]{1,0:T(4,128)S(1)}, f32[8,128]{1,0:T(8,128)S(1)}) custom-call(bf16[5,4,2048]{2,1,0:T(4,128)(2,1)} %bitcast.4, f32[1,2048]{1,0:T(1,128)} %bitcast.5, f32[4]{0:T(128)} %t_hbm.1, s32[4,4]{1,0:T(4,128)} %dt_hbm.1, bf16[37984,2048]{1,0:T(8,128)(2,1)} %bitcast.2.w_ref, ...), custom_call_target="tpu_custom_call" | custom-call | tf_op jit(solution)/shard_map/verify/pallas_call | solution.py:426
  41.1 1.7 %finish.1 = (f32[4,4]{1,0:T(4,128)}, f32[4,4]{1,0:T(4,128)}, f32[4,4,37984]{2,1,0:T(4,128)}, f32[1,4]{1,0:T(1,128)}) custom-call(f32[4,4,37984]{2,1,0:T(4,128)S(1)} %get-tuple-element.12.ex_ref, f32[4,128]{1,0:T(4,128)S(1)} %get-tuple-element.13.norm_ref, f32[4,128]{1,0:T(4,128)S(1)} %get-tuple-element.14.acc_ref, f32[8,128]{1,0:T(8,128)S(1)} %get-tuple-element.15.lse_ref), custom_call_target="tpu_custom_call" | custom-call | tf_op jit(solution)/shard_map/finish/pallas_call | solution.py:470
where the time goes:
time: 42.9 us; the launch traced here: 42.8 us
  Pallas kernels  42.1 us (98%)
  between operations  0.64 us (1%)
    pallas_call x1, Pallas kernels, local_step(): pl.pallas_call(verify_kernel, out_shape=[vmem((4, 4, n_ids), F32), vmem((...  40.5 us
    pallas_call x1, Pallas kernels, local_step(): pl.pallas_call(finish_kernel, out_shape=[jax.ShapeDtypeStruct((4, 4), F32...  1.68 us

commit v1 on v0

--- a/solution.py
+++ b/solution.py
@@ -17,7 +17,7 @@
 FIRST = 6
 HELD = 2
 RELAY = 4
-PARTS = 2
+PARTS = 1
 PASS = 2048
 
 
@@ -261,7 +261,7 @@
     lax.fori_loop(FIRST + SHARED, steps - 1, lambda i, _: step(i, 32), None)
     end, slot = steps - 1, (steps - 1) % SLOTS
     copies = tile_copies(end, slot)
-    for lo, size in ((0, part), (part, part)):
+    for lo, size in [(k * part, part) for k in range(PARTS)]:
         for c in copies[lo // part : (lo + size) // part]:
             c.wait()
         consume(slot, column(end), lo, size, 32, 0)

time: 42.9 us -> 42.9 us (level)
  no operation moved by 1% of the time
where the time goes in v1:
time: 42.9 us; the launch traced here: 42.8 us
  Pallas kernels  42.1 us (98%)
  between operations  0.64 us (1%)
    pallas_call x1, Pallas kernels, local_step(): pl.pallas_call(verify_kernel, out_shape=[vmem((4, 4, n_ids), F32), vmem((...  40.4 us
    pallas_call x1, Pallas kernels, local_step(): pl.pallas_call(finish_kernel, out_shape=[jax.ShapeDtypeStruct((4, 4), F32...  1.68 us

profile of v1, /device:TPU:0, one launch (start us, length us, event | category | flops | bytes accessed | tf_op | source)
XLA Modules:
  0.0 42.8 jit_solution(9927283268595349082)
XLA Ops:
  0.6 40.4 %verify.1 = (f32[4,4,37984]{2,1,0:T(4,128)S(1)}, f32[4,128]{1,0:T(4,128)S(1)}, f32[4,128]{1,0:T(4,128)S(1)}, f32[8,128]{1,0:T(8,128)S(1)}) custom-call(bf16[5,4,2048]{2,1,0:T(4,128)(2,1)} %bitcast.4, f32[1,2048]{1,0:T(1,128)} %bitcast.5, f32[4]{0:T(128)} %t_hbm.1, s32[4,4]{1,0:T(4,128)} %dt_hbm.1, bf16[37984,2048]{1,0:T(8,128)(2,1)} %bitcast.2.w_ref, ...), custom_call_target="tpu_custom_call" | custom-call | tf_op jit(solution)/shard_map/verify/pallas_call | solution.py:426
  41.1 1.7 %finish.1 = (f32[4,4]{1,0:T(4,128)}, f32[4,4]{1,0:T(4,128)}, f32[4,4,37984]{2,1,0:T(4,128)}, f32[1,4]{1,0:T(1,128)}) custom-call(f32[4,4,37984]{2,1,0:T(4,128)S(1)} %get-tuple-element.12.ex_ref, f32[4,128]{1,0:T(4,128)S(1)} %get-tuple-element.13.norm_ref, f32[4,128]{1,0:T(4,128)S(1)} %get-tuple-element.14.acc_ref, f32[8,128]{1,0:T(8,128)S(1)} %get-tuple-element.15.lse_ref), custom_call_target="tpu_custom_call" | custom-call | tf_op jit(solution)/shard_map/finish/pallas_call | solution.py:470

commit v2 on v1

--- a/solution.py
+++ b/solution.py
@@ -13,8 +13,8 @@
 SUB = 256
 DEPTH = 256
 SLOTS = 3
-SHARED = 14
-FIRST = 6
+SHARED = 15
+FIRST = 5
 HELD = 2
 RELAY = 4
 PARTS = 1

time: 42.9 us -> 43.2 us (level)
  no operation moved by 1% of the time
where the time goes in v2:
time: 43.2 us; the launch traced here: 43.1 us
  Pallas kernels  42.4 us (98%)
  between operations  0.64 us (1%)
    pallas_call x1, Pallas kernels, local_step(): pl.pallas_call(verify_kernel, out_shape=[vmem((4, 4, n_ids), F32), vmem((...  40.7 us
    pallas_call x1, Pallas kernels, local_step(): pl.pallas_call(finish_kernel, out_shape=[jax.ShapeDtypeStruct((4, 4), F32...  1.68 us

profile of v2, /device:TPU:0, one launch (start us, length us, event | category | flops | bytes accessed | tf_op | source)
XLA Modules:
  0.0 43.1 jit_solution(12918202157778929084)
XLA Ops:
  0.6 40.7 %verify.1 = (f32[4,4,37984]{2,1,0:T(4,128)S(1)}, f32[4,128]{1,0:T(4,128)S(1)}, f32[4,128]{1,0:T(4,128)S(1)}, f32[8,128]{1,0:T(8,128)S(1)}) custom-call(bf16[5,4,2048]{2,1,0:T(4,128)(2,1)} %bitcast.4, f32[1,2048]{1,0:T(1,128)} %bitcast.5, f32[4]{0:T(128)} %t_hbm.1, s32[4,4]{1,0:T(4,128)} %dt_hbm.1, bf16[37984,2048]{1,0:T(8,128)(2,1)} %bitcast.2.w_ref, ...), custom_call_target="tpu_custom_call" | custom-call | tf_op jit(solution)/shard_map/verify/pallas_call | solution.py:426
  41.4 1.7 %finish.1 = (f32[4,4]{1,0:T(4,128)}, f32[4,4]{1,0:T(4,128)}, f32[4,4,37984]{2,1,0:T(4,128)}, f32[1,4]{1,0:T(1,128)}) custom-call(f32[4,4,37984]{2,1,0:T(4,128)S(1)} %get-tuple-element.12.ex_ref, f32[4,128]{1,0:T(4,128)S(1)} %get-tuple-element.13.norm_ref, f32[4,128]{1,0:T(4,128)S(1)} %get-tuple-element.14.acc_ref, f32[8,128]{1,0:T(8,128)S(1)} %get-tuple-element.15.lse_ref), custom_call_target="tpu_custom_call" | custom-call | tf_op jit(solution)/shard_map/finish/pallas_call | solution.py:470

commit v3 on v2

--- a/solution.py
+++ b/solution.py
@@ -14,9 +14,10 @@
 DEPTH = 256
 SLOTS = 3
 SHARED = 15
-FIRST = 5
+FIRST = 4
+LATE = 5
 HELD = 2
-RELAY = 4
+RELAY = 3
 PARTS = 1
 PASS = 2048
 
@@ -324,17 +325,21 @@
     for c in e3:
         c.start()
 
-    def take_z(k, _):
+    def theirs_at(k):
+        return pl.multiple_of((FIRST + (1 - dp) * SHARED + k) * TILE, TILE)
+
+    def await_z(k):
         z_copy(k).wait_send()
-        at = pl.multiple_of((FIRST + (1 - dp) * SHARED + k) * TILE, TILE)
         pltpu.make_async_remote_copy(
-            src_ref=zsend.at[k], dst_ref=s_scr.at[:, :, pl.ds(at, TILE)], send_sem=zs_sem.at[k], recv_sem=zr_sem.at[k],
-            device_id=partner, device_id_type=MESH,
+            src_ref=zsend.at[k], dst_ref=s_scr.at[:, :, pl.ds(theirs_at(k), TILE)],
+            send_sem=zs_sem.at[k], recv_sem=zr_sem.at[k], device_id=partner, device_id_type=MESH,
         ).wait_recv()
-        prepare(at, TILE)
-
-    lax.fori_loop(0, SHARED, take_z, None)
-
+
+    def take_early(k, _):
+        await_z(k)
+        prepare(theirs_at(k), TILE)
+
+    lax.fori_loop(0, SHARED - LATE, take_early, None)
     for c in e1:
         c.wait()
     lses = [near] + [e1r[d] for d in range(3)]
@@ -342,28 +347,36 @@
     sums = jnp.exp(lses[0] - top) + jnp.exp(lses[1] - top) + jnp.exp(lses[2] - top) + jnp.exp(lses[3] - top)
     lse = top + jnp.log(sums)
     lse_ref[...] = lse
-    scale = [jnp.exp(row_m[b] - jnp.broadcast_to(unpack(lse[0:4, :], b), (4, 128))) for b in range(4)]
-
-    def excess(b, at, size):
-        e = jnp.maximum(s_scr[b, :, pl.ds(at, size)] * scale[b][:, :size] - qv[b, :, pl.ds(at, size)], 0.0)
+    row_l = [jnp.broadcast_to(unpack(lse[0:4, :], b), (4, 128)) for b in range(4)]
+    scale = [jnp.exp(row_m[b] - row_l[b]) for b in range(4)]
+
+    def excess(b, at, size, p):
+        e = jnp.maximum(p - qv[b, :, pl.ds(at, size)], 0.0)
         ex_ref[b, :, pl.ds(at, size)] = e
         return e
 
-    def last_pass(at, size, sums):
+    def close(at, sums, prepared):
         out = []
         for b in range(4):
             acc = sums[b]
-            for off in range(0, size, 128):
-                acc = acc + excess(b, at + off, 128)
+            for off in range(0, TILE, 128):
+                v = s_scr[b, :, pl.ds(at + off, 128)]
+                acc = acc + excess(b, at + off, 128, v * scale[b] if prepared else jnp.exp(v - row_l[b]))
             out.append(acc)
         return tuple(out)
 
-    sums = lax.fori_loop(0, whole // PASS, lambda i, t: last_pass(pl.multiple_of(i * PASS, 128), PASS, t), (zero,) * 4)
-    sums = last_pass(whole, tail_at - whole, sums)
+    def close_late(k, sums):
+        await_z(k)
+        return close(theirs_at(k), sums, False)
+
+    sums = lax.fori_loop(0, steps, lambda i, t: close(column(i), t, True), (zero,) * 4)
     rows = []
     for b in range(4):
-        e = excess(b, tail_at, tail)
-        rows.append(jnp.sum(sums[b], axis=1, keepdims=True) + jnp.sum(e, axis=1, keepdims=True))
+        e = excess(b, tail_at, tail, s_scr[b, :, tail_at : tail_at + tail] * scale[b][:, :tail])
+        rows.append(jnp.sum(e, axis=1, keepdims=True))
+    sums = lax.fori_loop(0, SHARED - LATE, lambda k, t: close(theirs_at(k), t, True), sums)
+    sums = lax.fori_loop(SHARED - LATE, SHARED, close_late, sums)
+    rows = [jnp.sum(sums[b], axis=1, keepdims=True) + rows[b] for b in range(4)]
     e2s[...] = pack(rows)
     e2 = exchange(e2s, e2r, e2_sem)
     for c in e2:

time: 43.2 us -> 42 us (0.972)
  Pallas kernels: 42.4 us -> 41.3 us
    pallas_call x1, Pallas kernels: 40.7 us -> 39.6 us  [local_step(): pl.pallas_call(verify_kernel, out_shape=[vmem((4, 4, n_ids), F32), vmem((...]
where the time goes in v3:
time: 42 us; the launch traced here: 41.9 us
  Pallas kernels  41.3 us (98%)
  between operations  0.64 us (2%)
    pallas_call x1, Pallas kernels, local_step(): pl.pallas_call(verify_kernel, out_shape=[vmem((4, 4, n_ids), F32), vmem((...  39.6 us
    pallas_call x1, Pallas kernels, local_step(): pl.pallas_call(finish_kernel, out_shape=[jax.ShapeDtypeStruct((4, 4), F32...  1.68 us

profile of v3, /device:TPU:0, one launch (start us, length us, event | category | flops | bytes accessed | tf_op | source)
XLA Modules:
  0.0 41.9 jit_solution(10406141998477996472)
XLA Ops:
  0.6 39.6 %verify.1 = (f32[4,4,37984]{2,1,0:T(4,128)S(1)}, f32[4,128]{1,0:T(4,128)S(1)}, f32[4,128]{1,0:T(4,128)S(1)}, f32[8,128]{1,0:T(8,128)S(1)}) custom-call(bf16[5,4,2048]{2,1,0:T(4,128)(2,1)} %bitcast.4, f32[1,2048]{1,0:T(1,128)} %bitcast.5, f32[4]{0:T(128)} %t_hbm.1, s32[4,4]{1,0:T(4,128)} %dt_hbm.1, bf16[37984,2048]{1,0:T(8,128)(2,1)} %bitcast.2.w_ref, ...), custom_call_target="tpu_custom_call" | custom-call | tf_op jit(solution)/shard_map/verify/pallas_call | solution.py:439
  40.2 1.7 %finish.1 = (f32[4,4]{1,0:T(4,128)}, f32[4,4]{1,0:T(4,128)}, f32[4,4,37984]{2,1,0:T(4,128)}, f32[1,4]{1,0:T(1,128)}) custom-call(f32[4,4,37984]{2,1,0:T(4,128)S(1)} %get-tuple-element.12.ex_ref, f32[4,128]{1,0:T(4,128)S(1)} %get-tuple-element.13.norm_ref, f32[4,128]{1,0:T(4,128)S(1)} %get-tuple-element.14.acc_ref, f32[8,128]{1,0:T(8,128)S(1)} %get-tuple-element.15.lse_ref), custom_call_target="tpu_custom_call" | custom-call | tf_op jit(solution)/shard_map/finish/pallas_call | solution.py:483

commit v4 on v3

--- a/solution.py
+++ b/solution.py
@@ -98,6 +98,27 @@
         for k in range(0, width, 128):
             xt[k : k + 128, at : at + 32] = xrows[:, k : k + 128].T.astype(jnp.bfloat16)
 
+    pl.semaphore_wait(barrier, 4)
+    core = lax.rem(tp, 2)
+    sibling = (dp, tp + 1 - 2 * core)
+
+    def width_half(ref, c):
+        return ref.at[:, :, pl.ds(pl.multiple_of(c * (width // 2), width // 2), width // 2)]
+
+    def x_copy(src, c, to, k):
+        return pltpu.make_async_remote_copy(
+            src_ref=width_half(src, c), dst_ref=width_half(xp, c), send_sem=x_sem.at[0, k], recv_sem=x_sem.at[1, k],
+            device_id=to, device_id_type=MESH,
+        )
+
+    x_direct = x_copy(xf, core, partner, 0)
+    x_relay = x_copy(xp, core, sibling, 1)
+    t_copy = pltpu.make_async_remote_copy(
+        src_ref=tv, dst_ref=tp_recv, send_sem=t_sem.at[0], recv_sem=t_sem.at[1], device_id=partner, device_id_type=MESH
+    )
+    x_direct.start()
+    t_copy.start()
+
     xt[:, 32:128] = jnp.zeros((width, 96), jnp.bfloat16)
     xb[32:64, :] = jnp.zeros((32, width), jnp.bfloat16)
     lay_rows(xf, tv, 0)
@@ -107,27 +128,6 @@
     m_scr[...] = jnp.full(m_scr.shape, LOWEST, F32)
     l_scr[...] = jnp.zeros_like(l_scr)
     k_scr[...] = jnp.zeros_like(k_scr)
-
-    pl.semaphore_wait(barrier, 4)
-    core = lax.rem(tp, 2)
-    sibling = (dp, tp + 1 - 2 * core)
-
-    def width_half(ref, c):
-        return ref.at[:, :, pl.ds(pl.multiple_of(c * (width // 2), width // 2), width // 2)]
-
-    def x_copy(src, c, to, k):
-        return pltpu.make_async_remote_copy(
-            src_ref=width_half(src, c), dst_ref=width_half(xp, c), send_sem=x_sem.at[0, k], recv_sem=x_sem.at[1, k],
-            device_id=to, device_id_type=MESH,
-        )
-
-    x_direct = x_copy(xf, core, partner, 0)
-    x_relay = x_copy(xp, core, sibling, 1)
-    t_copy = pltpu.make_async_remote_copy(
-        src_ref=tv, dst_ref=tp_recv, send_sem=t_sem.at[0], recv_sem=t_sem.at[1], device_id=partner, device_id_type=MESH
-    )
-    x_direct.start()
-    t_copy.start()
 
     def by_rows(w, depth):
         return lax.dot_general(xb[:, depth], w, (((1,), (1,)), ((), ())), preferred_element_type=F32)
@@ -369,12 +369,17 @@
         await_z(k)
         return close(theirs_at(k), sums, False)
 
-    sums = lax.fori_loop(0, steps, lambda i, t: close(column(i), t, True), (zero,) * 4)
+    def close_from(first, count, sums):
+        return lax.fori_loop(0, count, lambda i, t: close(pl.multiple_of((first + i) * TILE, TILE), t, True), sums)
+
+    sums = close_from(0, FIRST, (zero,) * 4)
+    sums = close_from(FIRST + dp * SHARED, SHARED, sums)
+    sums = close_from(FIRST + 2 * SHARED, last, sums)
     rows = []
     for b in range(4):
         e = excess(b, tail_at, tail, s_scr[b, :, tail_at : tail_at + tail] * scale[b][:, :tail])
         rows.append(jnp.sum(e, axis=1, keepdims=True))
-    sums = lax.fori_loop(0, SHARED - LATE, lambda k, t: close(theirs_at(k), t, True), sums)
+    sums = close_from(FIRST + (1 - dp) * SHARED, SHARED - LATE, sums)
     sums = lax.fori_loop(SHARED - LATE, SHARED, close_late, sums)
     rows = [jnp.sum(sums[b], axis=1, keepdims=True) + rows[b] for b in range(4)]
     e2s[...] = pack(rows)

time: 42 us -> 41.7 us (level)
  no operation moved by 1% of the time
where the time goes in v4:
time: 41.7 us; the launch traced here: 41.6 us
  Pallas kernels  41 us (98%)
  between operations  0.64 us (2%)
    pallas_call x1, Pallas kernels, local_step(): pl.pallas_call(verify_kernel, out_shape=[vmem((4, 4, n_ids), F32), vmem((...  39.3 us
    pallas_call x1, Pallas kernels, local_step(): pl.pallas_call(finish_kernel, out_shape=[jax.ShapeDtypeStruct((4, 4), F32...  1.68 us

profile of v4, /device:TPU:0, one launch (start us, length us, event | category | flops | bytes accessed | tf_op | source)
XLA Modules:
  0.0 41.6 jit_solution(12421060753201331282)
XLA Ops:
  0.6 39.3 %verify.1 = (f32[4,4,37984]{2,1,0:T(4,128)S(1)}, f32[4,128]{1,0:T(4,128)S(1)}, f32[4,128]{1,0:T(4,128)S(1)}, f32[8,128]{1,0:T(8,128)S(1)}) custom-call(bf16[5,4,2048]{2,1,0:T(4,128)(2,1)} %bitcast.4, f32[1,2048]{1,0:T(1,128)} %bitcast.5, f32[4]{0:T(128)} %t_hbm.1, s32[4,4]{1,0:T(4,128)} %dt_hbm.1, bf16[37984,2048]{1,0:T(8,128)(2,1)} %bitcast.2.w_ref, ...), custom_call_target="tpu_custom_call" | custom-call | tf_op jit(solution)/shard_map/verify/pallas_call | solution.py:444
  40.0 1.7 %finish.1 = (f32[4,4]{1,0:T(4,128)}, f32[4,4]{1,0:T(4,128)}, f32[4,4,37984]{2,1,0:T(4,128)}, f32[1,4]{1,0:T(1,128)}) custom-call(f32[4,4,37984]{2,1,0:T(4,128)S(1)} %get-tuple-element.12.ex_ref, f32[4,128]{1,0:T(4,128)S(1)} %get-tuple-element.13.norm_ref, f32[4,128]{1,0:T(4,128)S(1)} %get-tuple-element.14.acc_ref, f32[8,128]{1,0:T(8,128)S(1)} %get-tuple-element.15.lse_ref), custom_call_target="tpu_custom_call" | custom-call | tf_op jit(solution)/shard_map/finish/pallas_call | solution.py:488

commit v5 on v4

--- a/solution.py
+++ b/solution.py
@@ -13,10 +13,10 @@
 SUB = 256
 DEPTH = 256
 SLOTS = 3
-SHARED = 15
+SHARED = 16
 FIRST = 4
-LATE = 5
-HELD = 2
+LATE = 6
+HELD = 3
 RELAY = 3
 PARTS = 1
 PASS = 2048

time: 41.7 us -> 42.1 us (level)
  no operation moved by 1% of the time
where the time goes in v5:
time: 42.1 us; the launch traced here: 42 us
  Pallas kernels  41.4 us (98%)
  between operations  0.64 us (2%)
    pallas_call x1, Pallas kernels, local_step(): pl.pallas_call(verify_kernel, out_shape=[vmem((4, 4, n_ids), F32), vmem((...  39.7 us
    pallas_call x1, Pallas kernels, local_step(): pl.pallas_call(finish_kernel, out_shape=[jax.ShapeDtypeStruct((4, 4), F32...  1.68 us

profile of v5, /device:TPU:0, one launch (start us, length us, event | category | flops | bytes accessed | tf_op | source)
XLA Modules:
  0.0 42.0 jit_solution(1714210924974613216)
XLA Ops:
  0.6 39.7 %verify.1 = (f32[4,4,37984]{2,1,0:T(4,128)S(1)}, f32[4,128]{1,0:T(4,128)S(1)}, f32[4,128]{1,0:T(4,128)S(1)}, f32[8,128]{1,0:T(8,128)S(1)}) custom-call(bf16[5,4,2048]{2,1,0:T(4,128)(2,1)} %bitcast.4, f32[1,2048]{1,0:T(1,128)} %bitcast.5, f32[4]{0:T(128)} %t_hbm.1, s32[4,4]{1,0:T(4,128)} %dt_hbm.1, bf16[37984,2048]{1,0:T(8,128)(2,1)} %bitcast.2.w_ref, ...), custom_call_target="tpu_custom_call" | custom-call | tf_op jit(solution)/shard_map/verify/pallas_call | solution.py:444
  40.3 1.7 %finish.1 = (f32[4,4]{1,0:T(4,128)}, f32[4,4]{1,0:T(4,128)}, f32[4,4,37984]{2,1,0:T(4,128)}, f32[1,4]{1,0:T(1,128)}) custom-call(f32[4,4,37984]{2,1,0:T(4,128)S(1)} %get-tuple-element.12.ex_ref, f32[4,128]{1,0:T(4,128)S(1)} %get-tuple-element.13.norm_ref, f32[4,128]{1,0:T(4,128)S(1)} %get-tuple-element.14.acc_ref, f32[8,128]{1,0:T(8,128)S(1)} %get-tuple-element.15.lse_ref), custom_call_target="tpu_custom_call" | custom-call | tf_op jit(solution)/shard_map/finish/pallas_call | solution.py:488

commit v6 on v4

--- a/solution.py
+++ b/solution.py
@@ -18,7 +18,7 @@
 LATE = 5
 HELD = 2
 RELAY = 3
-PARTS = 1
+PARTS = 2
 PASS = 2048
 
 
@@ -207,8 +207,15 @@
 
         @pl.when(i + SLOTS < steps)
         def _():
-            for c in tile_copies(i + SLOTS, slot):
-                c.start()
+            tile_copies(i + SLOTS, slot)[0].start()
+
+        @pl.when(i + SLOTS < steps - 1)
+        def _():
+            tile_copies(i + SLOTS, slot)[1].start()
+
+        @pl.when(i + SLOTS == steps)
+        def _():
+            tile_copies(steps - 1, (steps - 1) % SLOTS)[1].start()
 
         if rows == 64:
 

time: 41.7 us -> 41.8 us (level)
  no operation moved by 1% of the time
where the time goes in v6:
time: 41.8 us; the launch traced here: 41.7 us
  Pallas kernels  41 us (98%)
  between operations  0.64 us (2%)
    pallas_call x1, Pallas kernels, local_step(): pl.pallas_call(verify_kernel, out_shape=[vmem((4, 4, n_ids), F32), vmem((...  39.4 us
    pallas_call x1, Pallas kernels, local_step(): pl.pallas_call(finish_kernel, out_shape=[jax.ShapeDtypeStruct((4, 4), F32...  1.68 us

profile of v6, /device:TPU:0, one launch (start us, length us, event | category | flops | bytes accessed | tf_op | source)
XLA Modules:
  0.0 41.7 jit_solution(2675556468916238218)
XLA Ops:
  0.6 39.4 %verify.1 = (f32[4,4,37984]{2,1,0:T(4,128)S(1)}, f32[4,128]{1,0:T(4,128)S(1)}, f32[4,128]{1,0:T(4,128)S(1)}, f32[8,128]{1,0:T(8,128)S(1)}) custom-call(bf16[5,4,2048]{2,1,0:T(4,128)(2,1)} %bitcast.4, f32[1,2048]{1,0:T(1,128)} %bitcast.5, f32[4]{0:T(128)} %t_hbm.1, s32[4,4]{1,0:T(4,128)} %dt_hbm.1, bf16[37984,2048]{1,0:T(8,128)(2,1)} %bitcast.2.w_ref, ...), custom_call_target="tpu_custom_call" | custom-call | tf_op jit(solution)/shard_map/verify/pallas_call | solution.py:451
  40.0 1.7 %finish.1 = (f32[4,4]{1,0:T(4,128)}, f32[4,4]{1,0:T(4,128)}, f32[4,4,37984]{2,1,0:T(4,128)}, f32[1,4]{1,0:T(1,128)}) custom-call(f32[4,4,37984]{2,1,0:T(4,128)S(1)} %get-tuple-element.12.ex_ref, f32[4,128]{1,0:T(4,128)S(1)} %get-tuple-element.13.norm_ref, f32[4,128]{1,0:T(4,128)S(1)} %get-tuple-element.14.acc_ref, f32[8,128]{1,0:T(8,128)S(1)} %get-tuple-element.15.lse_ref), custom_call_target="tpu_custom_call" | custom-call | tf_op jit(solution)/shard_map/finish/pallas_call | solution.py:495

commit v7 on v4

--- a/solution.py
+++ b/solution.py
@@ -14,10 +14,10 @@
 DEPTH = 256
 SLOTS = 3
 SHARED = 15
-FIRST = 4
+FIRST = 3
 LATE = 5
-HELD = 2
-RELAY = 3
+HELD = 3
+RELAY = 2
 PARTS = 1
 PASS = 2048
 

time: 41.7 us -> 42.4 us (1.017)
  Pallas kernels: 41 us -> 41.6 us
    pallas_call x1, Pallas kernels: 39.3 us -> 39.9 us  [local_step(): pl.pallas_call(verify_kernel, out_shape=[vmem((4, 4, n_ids), F32), vmem((...]
where the time goes in v7:
time: 42.4 us; the launch traced here: 42.3 us
  Pallas kernels  41.6 us (98%)
  between operations  0.64 us (2%)
    pallas_call x1, Pallas kernels, local_step(): pl.pallas_call(verify_kernel, out_shape=[vmem((4, 4, n_ids), F32), vmem((...  39.9 us
    pallas_call x1, Pallas kernels, local_step(): pl.pallas_call(finish_kernel, out_shape=[jax.ShapeDtypeStruct((4, 4), F32...  1.68 us

profile of v7, /device:TPU:0, one launch (start us, length us, event | category | flops | bytes accessed | tf_op | source)
XLA Modules:
  0.0 42.3 jit_solution(591932095231746740)
XLA Ops:
  0.6 39.9 %verify.1 = (f32[4,4,37984]{2,1,0:T(4,128)S(1)}, f32[4,128]{1,0:T(4,128)S(1)}, f32[4,128]{1,0:T(4,128)S(1)}, f32[8,128]{1,0:T(8,128)S(1)}) custom-call(bf16[5,4,2048]{2,1,0:T(4,128)(2,1)} %bitcast.4, f32[1,2048]{1,0:T(1,128)} %bitcast.5, f32[4]{0:T(128)} %t_hbm.1, s32[4,4]{1,0:T(4,128)} %dt_hbm.1, bf16[37984,2048]{1,0:T(8,128)(2,1)} %bitcast.2.w_ref, ...), custom_call_target="tpu_custom_call" | custom-call | tf_op jit(solution)/shard_map/verify/pallas_call | solution.py:444
  40.6 1.7 %finish.1 = (f32[4,4]{1,0:T(4,128)}, f32[4,4]{1,0:T(4,128)}, f32[4,4,37984]{2,1,0:T(4,128)}, f32[1,4]{1,0:T(1,128)}) custom-call(f32[4,4,37984]{2,1,0:T(4,128)S(1)} %get-tuple-element.12.ex_ref, f32[4,128]{1,0:T(4,128)S(1)} %get-tuple-element.13.norm_ref, f32[4,128]{1,0:T(4,128)S(1)} %get-tuple-element.14.acc_ref, f32[8,128]{1,0:T(8,128)S(1)} %get-tuple-element.15.lse_ref), custom_call_target="tpu_custom_call" | custom-call | tf_op jit(solution)/shard_map/finish/pallas_call | solution.py:488

commit v8 on v4

--- a/solution.py
+++ b/solution.py
@@ -16,7 +16,7 @@
 SHARED = 15
 FIRST = 4
 LATE = 5
-HELD = 2
+HELD = 3
 RELAY = 3
 PARTS = 1
 PASS = 2048

time: 41.7 us -> 40.8 us (0.978)
  Pallas kernels: 41 us -> 40.1 us
    pallas_call x1, Pallas kernels: 39.3 us -> 38.4 us  [local_step(): pl.pallas_call(verify_kernel, out_shape=[vmem((4, 4, n_ids), F32), vmem((...]
where the time goes in v8:
time: 40.8 us; the launch traced here: 40.7 us
  Pallas kernels  40.1 us (98%)
  between operations  0.64 us (2%)
    pallas_call x1, Pallas kernels, local_step(): pl.pallas_call(verify_kernel, out_shape=[vmem((4, 4, n_ids), F32), vmem((...  38.4 us
    pallas_call x1, Pallas kernels, local_step(): pl.pallas_call(finish_kernel, out_shape=[jax.ShapeDtypeStruct((4, 4), F32...  1.68 us

profile of v8, /device:TPU:0, one launch (start us, length us, event | category | flops | bytes accessed | tf_op | source)
XLA Modules:
  0.0 40.7 jit_solution(12212412626853754016)
XLA Ops:
  0.6 38.4 %verify.1 = (f32[4,4,37984]{2,1,0:T(4,128)S(1)}, f32[4,128]{1,0:T(4,128)S(1)}, f32[4,128]{1,0:T(4,128)S(1)}, f32[8,128]{1,0:T(8,128)S(1)}) custom-call(bf16[5,4,2048]{2,1,0:T(4,128)(2,1)} %bitcast.4, f32[1,2048]{1,0:T(1,128)} %bitcast.5, f32[4]{0:T(128)} %t_hbm.1, s32[4,4]{1,0:T(4,128)} %dt_hbm.1, bf16[37984,2048]{1,0:T(8,128)(2,1)} %bitcast.2.w_ref, ...), custom_call_target="tpu_custom_call" | custom-call | tf_op jit(solution)/shard_map/verify/pallas_call | solution.py:444
  39.0 1.7 %finish.1 = (f32[4,4]{1,0:T(4,128)}, f32[4,4]{1,0:T(4,128)}, f32[4,4,37984]{2,1,0:T(4,128)}, f32[1,4]{1,0:T(1,128)}) custom-call(f32[4,4,37984]{2,1,0:T(4,128)S(1)} %get-tuple-element.12.ex_ref, f32[4,128]{1,0:T(4,128)S(1)} %get-tuple-element.13.norm_ref, f32[4,128]{1,0:T(4,128)S(1)} %get-tuple-element.14.acc_ref, f32[8,128]{1,0:T(8,128)S(1)} %get-tuple-element.15.lse_ref), custom_call_target="tpu_custom_call" | custom-call | tf_op jit(solution)/shard_map/finish/pallas_call | solution.py:488
